TPU v7x, 128 devices: a whole 4x4x4 slice. The times are simulated.
128 devices in a mesh: dp: 1, ep: 128 (over z, y, x, core).
Axes of the slice: x: 4, y: 4, z: 4, core: 2. Of those that a mesh axis runs over, the one named last changes fastest.
Arguments:
- x: bfloat16 [128, 64, 2048], P(('dp', 'ep'))
- idx: int32 [128, 64, 8], P(('dp', 'ep'))
- gates: float32 [128, 64, 8], P(('dp', 'ep'))
- g1: float32 [2048], replicated
- wq: bfloat16 [2048, 4096], replicated
- wk: bfloat16 [2048, 4096], replicated
- wv: bfloat16 [2048, 4096], replicated
- wo: bfloat16 [4096, 2048], replicated
- g2: float32 [2048], replicated
- w1: bfloat16 [128, 2048, 768], P('ep')
- w3: bfloat16 [128, 2048, 768], P('ep')
- w2: bfloat16 [128, 768, 2048], P('ep')
Outputs:
- output: bfloat16 [128, 64, 2048], P(('dp', 'ep'))
All inputs are finite; a program needn't handle non-finite values.
Results may differ from a plain program's by a relative error of at most 0.0112406.
Values are sent between devices in bfloat16 or wider.
A program may use at most 1 GiB of HBM per device.

v0:
```python
import jax
import jax.numpy as jnp
from jax import lax
from jax.sharding import PartitionSpec as P

EPS = 1e-6
HEAD = 128


def rms(x, g):
    xf = x.astype(jnp.float32)
    return (xf * lax.rsqrt(jnp.mean(xf * xf, axis=-1, keepdims=True) + EPS) * g).astype(jnp.bfloat16)


def attend(q, k, v):
    n = q.shape[0]
    s = jnp.einsum('qhd,khd->hqk', q, k, preferred_element_type=jnp.float32) * q.shape[-1] ** -0.5
    mask = jnp.arange(n)[:, None] >= jnp.arange(n)[None, :]
    s = jnp.where(mask[None], s, -1e30)
    p = jax.nn.softmax(s, axis=-1).astype(jnp.bfloat16)
    return jnp.einsum('hqk,khd->qhd', p, v, preferred_element_type=jnp.float32).astype(jnp.bfloat16)


def slot_pos(flat, n_exp):
    n = flat.shape[0]
    order = jnp.argsort(flat, stable=True)
    se = flat[order]
    counts = jnp.zeros((n_exp,), jnp.int32).at[flat].add(1)
    starts = jnp.cumsum(counts) - counts
    ps = jnp.arange(n, dtype=jnp.int32) - starts[se]
    return jnp.zeros((n,), jnp.int32).at[order].set(ps)


def solution(mesh):
    ep = mesh.shape['ep']
    tok = P(('dp', 'ep'))
    rep = P()
    exs = P('ep')

    def body(x, idx, gates, g1, wq, wk, wv, wo, g2, w1, w3, w2):
        n, s_len, d = x.shape
        t = n * s_len
        top = idx.shape[-1]
        g_loc = w1.shape[0]
        n_exp = g_loc * ep
        avg = top * t // n_exp
        cap = avg + avg // 2
        heads = wq.shape[1] // HEAD
        xf = x.reshape(t, d)
        xn = rms(xf, g1)

        def proj(w):
            return jnp.dot(xn, w, preferred_element_type=jnp.float32).astype(jnp.bfloat16).reshape(n, s_len, heads, HEAD)

        q = proj(wq)
        k = proj(wk)
        v = proj(wv)
        o = lax.map(lambda a: attend(a[0], a[1], a[2]), (q, k, v))
        att = jnp.dot(o.reshape(t, heads * HEAD), wo, preferred_element_type=jnp.float32).astype(jnp.bfloat16)
        h = (xf.astype(jnp.float32) + att.astype(jnp.float32)).astype(jnp.bfloat16)
        z = rms(h, g2)
        flat = idx.reshape(t * top)
        dest = flat * cap + slot_pos(flat, n_exp)
        buf = jnp.zeros((n_exp * cap, d), jnp.bfloat16).at[dest].set(jnp.repeat(z, top, axis=0))
        recv = lax.all_to_all(buf, 'ep', 0, 0, tiled=True)
        r = recv.reshape(ep, g_loc, cap, d).transpose(1, 0, 2, 3).reshape(g_loc, ep * cap, d)
        h1 = jnp.einsum('gnd,gdf->gnf', r, w1, preferred_element_type=jnp.float32)
        h3 = jnp.einsum('gnd,gdf->gnf', r, w3, preferred_element_type=jnp.float32)
        u = (jax.nn.silu(h1) * h3).astype(jnp.bfloat16)
        e_out = jnp.einsum('gnf,gfd->gnd', u, w2, preferred_element_type=jnp.float32).astype(jnp.bfloat16)
        e_out = e_out.reshape(g_loc, ep, cap, d).transpose(1, 0, 2, 3).reshape(ep * g_loc * cap, d)
        back = lax.all_to_all(e_out, 'ep', 0, 0, tiled=True)
        got = back[dest].reshape(t, top, d).astype(jnp.float32)
        moe = jnp.sum(got * gates.reshape(t, top, 1), axis=1)
        y = (h.astype(jnp.float32) + moe).astype(jnp.bfloat16)
        return y.reshape(n, s_len, d)

    return jax.shard_map(body, mesh=mesh, in_specs=(tok, tok, tok, rep, rep, rep, rep, rep, rep, exs, exs, exs), out_specs=tok, check_vma=False)
```

profile of v0, /device:TPU:1, one launch (start us, length us, event | category | flops | bytes accessed | tf_op | source)
XLA Modules:
  0.0 259.1 jit_solution(8360087455263453840)
XLA Ops:
  0.0 0.9 copy.24
  1.1 1.1 fusion.26
  2.3 9.1 %fusion.20 = bf16[8,32,8,128]{3,2,1,0:T(8,128)(2,1)S(1)} fusion(bf16[2048,4096]{1,0:T(8,128)(2,1)} %param.16, bf16[1,64,2048]{2,1,0:T(8,128)(2,1)} %param.12, f32[2048]{0:T(1024)} %param.15, f32[64]{0:T(128)S(1)} %add_rsqrt_fusion.1), kind=kOutput, calls=%fused_computation.33 | convolution fusion | flops 1074528256 | bytes 17572096 | tf_op jit(solution)/shard_map/dot_general | solution.py:53
  11.4 1.5 copy-done.1
  12.9 3.1 %fusion.21 = bf16[8,32,8,128]{3,2,1,0:T(8,128)(2,1)S(1)} fusion(bf16[2048,4096]{1,0:T(8,128)(2,1)S(1)} %copy-done.1, bf16[1,64,2048]{2,1,0:T(8,128)(2,1)S(1)} %copy-done.2, f32[2048]{0:T(1024)S(1)} %copy-done.3, f32[64]{0:T(128)S(1)} %add_rsqrt_fusion.1), kind=kOutput, calls=%fused_computation.34 | convolution fusion | flops 1074528256 | bytes 17572096 | tf_op jit(solution)/shard_map/dot_general | solution.py:53
  16.0 0.4 fusion.18
  16.5 1.0 copy-done.6
  17.5 0.3 fusion.48
  17.8 9.7 %fusion.19 = bf16[8,32,8,128]{3,2,1,0:T(8,128)(2,1)} fusion(bf16[2048,4096]{1,0:T(8,128)(2,1)} %param.18, bf16[1,64,2048]{2,1,0:T(8,128)(2,1)S(1)} %copy-done.2, f32[2048]{0:T(1024)S(1)} %copy-done.3, f32[64]{0:T(128)S(1)} %add_rsqrt_fusion.1), kind=kOutput, calls=%fused_computation.32 | convolution fusion | flops 1074528256 | bytes 17572096 | tf_op jit(solution)/shard_map/dot_general | solution.py:53
  27.5 3.0 %fusion.22 = bf16[32,8,8,128]{3,2,1,0:T(8,128)(2,1)} fusion(bf16[8,32,8,128]{3,2,1,0:T(8,128)(2,1)} %fusion.19, f32[32,64]{1,0:T(8,128)S(1)} %fusion.48, f32[32,64,64]{1,2,0:T(8,128)} %copy-done.6), kind=kOutput, calls=%fused_computation.35 | convolution fusion | flops 34211904 | bytes 1581056 | tf_op jit(solution)/shard_map/while/body/eval_jaxpr/hqk,khd->qhd/dot_general | solution.py:21
  30.5 9.9 %multiply_reduce_fusion = (f32[64]{0:T(128)S(1)}, f32[64,2048]{1,0:T(8,128)}) fusion(bf16[4096,2048]{1,0:T(8,128)(2,1)} %param.19, bf16[32,8,8,128]{3,2,1,0:T(8,128)(2,1)} %fusion.22, bf16[1,64,2048]{2,1,0:T(8,128)(2,1)S(1)} %copy-done.2), kind=kOutput, calls=%fused_computation.53 | convolution fusion | flops 1074790400 | bytes 18088192 | tf_op jit(solution)/shard_map/dot_general | solution.py:59
  40.4 3.8 %sort.17 = (s32[512]{0:T(512)}, s32[512]{0:T(512)S(1)}) sort(s32[512]{0:T(512)S(1)} %reshape.162, s32[512]{0:T(512)S(1)} %iota.24), dimensions={0}, to_apply=%region_3.4 | sort | flops 4608 | bytes 8192 | tf_op jit(solution)/shard_map/jit(argsort)/sort | solution.py:26
  44.2 3.7 %gather_fusion = s32[512]{0:T(512)S(1)} fusion(s32[512]{0:T(512)S(1)} %reshape.162, s32[1024]{0:T(1024)S(1)} %pad_clamp_fusion.2), kind=kCustom, calls=%fused_computation | custom fusion | bytes 6144 | tf_op jit(solution)/shard_map/gather | solution.py:27
  47.9 4.1 %scatter_custom_fusion = s32[128]{0:T(128)S(1)} fusion(s32[512]{0:T(512)S(1)} %bitcast.68, s32[512]{0:T(512)S(1)} %broadcast.97, s32[]{:T(128)} %constant.33.clone.1), kind=kCustom, calls=%fused_computation.70 | custom fusion | flops 512 | bytes 516 | tf_op jit(solution)/shard_map/scatter-add | solution.py:28
  52.0 0.1 copy.26
  52.1 0.2 reduce-window.9
  52.4 3.3 %gather_fusion.1 = s32[512]{0:T(512)S(1)} fusion(s32[128]{0:T(128)S(1)} %sub.20, s32[1024]{0:T(1024)S(1)} %pad_clamp_fusion.1), kind=kCustom, calls=%fused_computation.1 | custom fusion | bytes 6144 | tf_op jit(solution)/shard_map/gather | solution.py:30
  55.8 2.4 scatter_custom_fusion.1
  58.2 1.2 multiply_convert_fusion.1
  59.4 5.7 %scatter_custom_fusion.2 = bf16[768,2048]{1,0:T(8,128)(2,1)} fusion(s32[512]{0:T(512)S(1)} %compare_select_fusion.2, bf16[]{:T(256)} %constant.29.clone.1, bf16[64,2048]{1,0:T(8,128)(2,1)S(1)} %multiply_convert_fusion.1), kind=kCustom, calls=%fused_computation.24 | custom fusion | bytes 3407874 | tf_op jit(solution)/shard_map/scatter | solution.py:64
  65.1 6.2 %all_to_all.16 = bf16[128,6,2048]{2,1,0:T(8,128)(2,1)} reshape(bf16[768,2048]{1,0:T(8,128)(2,1)} %scatter_custom_fusion.2) | data formatting | bytes 6291456 | tf_op jit(solution)/shard_map/all_to_all | solution.py:65
  71.3 70.7 %all_to_all.24 = bf16[128,6,2048]{2,1,0:T(8,128)(2,1)} all-to-all(bf16[128,6,2048]{2,1,0:T(8,128)(2,1)} %all_to_all.16), channel_id=1, replica_groups=mesh['dp'=1,'ep'=128] {'ep'}, dimensions={0} | all-to-all | bytes 6291456 | tf_op jit(solution)/shard_map/all_to_all | solution.py:65
  142.1 6.3 %all_to_all.18 = bf16[768,2048]{1,0:T(8,128)(2,1)} reshape(bf16[128,6,2048]{2,1,0:T(8,128)(2,1)} %all_to_all.24) | data formatting | bytes 6291456 | tf_op jit(solution)/shard_map/all_to_all | solution.py:65
  148.4 6.9 %fusion.3 = f32[768,768]{1,0:T(8,128)} fusion(bf16[768,2048]{1,0:T(8,128)(2,1)} %all_to_all.18, bf16[1,2048,768]{2,1,0:T(8,128)(2,1)} %param.22), kind=kOutput, calls=%fused_computation.14 | convolution fusion | flops 2415919104 | bytes 8650752 | tf_op jit(solution)/shard_map/gnd,gdf->gnf/dot_general | solution.py:68
  155.3 11.0 %convolution_convert_fusion.3 = bf16[768,2048]{1,0:T(8,128)(2,1)} fusion(bf16[1,768,2048]{2,1,0:T(8,128)(2,1)S(1)} %copy-done, f32[768,768]{1,0:T(8,128)} %fusion.3, bf16[768,2048]{1,0:T(8,128)(2,1)} %all_to_all.18, bf16[1,2048,768]{2,1,0:T(8,128)(2,1)} %param.21), kind=kOutput, calls=%fused_computation.12 | convolution fusion | flops 4836950016 | bytes 14942208 | tf_op jit(solution)/shard_map/gnf,gfd->gnd/dot_general | solution.py:70
  166.3 6.3 %all_to_all.19 = bf16[128,6,2048]{2,1,0:T(8,128)(2,1)} reshape(bf16[768,2048]{1,0:T(8,128)(2,1)} %convolution_convert_fusion.3) | data formatting | bytes 6291456 | tf_op jit(solution)/shard_map/all_to_all | solution.py:72
  172.6 8.8 %all-to-all-start.1 = ((bf16[128,6,2048]{2,1,0:T(8,128)(2,1)}), bf16[128,6,2048]{2,1,0:T(8,128)(2,1)}, u32[]{:S(2)}, u32[]{:S(2)}) async-start(bf16[128,6,2048]{2,1,0:T(8,128)(2,1)} %all_to_all.19), calls=%async_computation.1 | async-start | bytes 8388608 | tf_op jit(solution)/shard_map/all_to_all | solution.py:72
  181.5 58.5 %all-to-all-done.1 = bf16[128,6,2048]{2,1,0:T(8,128)(2,1)} async-done(((bf16[128,6,2048]{2,1,0:T(8,128)(2,1)}), bf16[128,6,2048]{2,1,0:T(8,128)(2,1)}, u32[]{:S(2)}, u32[]{:S(2)}) %all-to-all-start.1) | async-done | bytes 3145760 | tf_op jit(solution)/shard_map/all_to_all | solution.py:72
  240.0 6.3 %all_to_all.21 = bf16[768,2048]{1,0:T(8,128)(2,1)} reshape(bf16[128,6,2048]{2,1,0:T(8,128)(2,1)} %all-to-all-done.1) | data formatting | bytes 6291456 | tf_op jit(solution)/shard_map/all_to_all | solution.py:72
  246.4 7.5 %gather_fusion.2 = bf16[512,2048]{1,0:T(8,128)(2,1)} fusion(bf16[768,2048]{1,0:T(8,128)(2,1)} %all_to_all.21, s32[1024]{0:T(1024)S(1)} %pad_clamp_fusion), kind=kCustom, calls=%fused_computation.2 | custom fusion | bytes 4196352 | tf_op jit(solution)/shard_map/gather | solution.py:73
  253.9 3.4 %fusion.1 = f32[64,2048]{1,0:T(8,128)S(1)} fusion(bf16[512,2048]{1,0:T(8,128)(2,1)} %gather_fusion.2, f32[64,8]{1,0:T(8,128)S(1)} %copy.27), kind=kLoop, calls=%fused_computation.11 | loop fusion | flops 3014656 | bytes 2623488 | tf_op jit(solution)/shard_map/reduce_sum | solution.py:74
  257.3 1.8 fusion.38
  (30 shorter events, 0.5 us)
Async XLA Ops:
  0.0 155.3 %copy-start = (bf16[1,768,2048]{2,1,0:T(8,128)(2,1)S(1)}, bf16[1,768,2048]{2,1,0:T(8,128)(2,1)}, u32[]{:S(2)}) copy-start(bf16[1,768,2048]{2,1,0:T(8,128)(2,1)} %param.23) | copy-start | bytes 9437188
  2.2 10.6 %copy-start.1 = (bf16[2048,4096]{1,0:T(8,128)(2,1)S(1)}, bf16[2048,4096]{1,0:T(8,128)(2,1)}, u32[]{:S(2)}) copy-start(bf16[2048,4096]{1,0:T(8,128)(2,1)} %param.17) | copy-start | bytes 50331652
  2.3 10.6 %copy-start.2 = (bf16[1,64,2048]{2,1,0:T(8,128)(2,1)S(1)}, bf16[1,64,2048]{2,1,0:T(8,128)(2,1)}, u32[]{:S(2)}) copy-start(bf16[1,64,2048]{2,1,0:T(8,128)(2,1)} %param.12) | copy-start | bytes 786436
  2.3 10.6 %copy-start.3 = (f32[2048]{0:T(1024)S(1)}, f32[2048]{0:T(1024)}, u32[]{:S(2)}) copy-start(f32[2048]{0:T(1024)} %param.15) | copy-start | bytes 24580
  16.5 1.0 copy-start.6
  40.4 17.9 %copy-start.4 = (f32[2048]{0:T(1024)S(1)}, f32[2048]{0:T(1024)}, u32[]{:S(2)}) copy-start(f32[2048]{0:T(1024)} %param.20) | copy-start | bytes 24580
  172.6 8.8 %copy-start.5 = (f32[1,64,8]{1,2,0:T(8,128)S(1)}, f32[1,64,8]{1,2,0:T(8,128)}, u32[]{:S(2)}) copy-start(f32[1,64,8]{1,2,0:T(8,128)} %param.14) | copy-start | bytes 6148
  172.6 67.5 %all-to-all-start.1 = ((bf16[128,6,2048]{2,1,0:T(8,128)(2,1)}), bf16[128,6,2048]{2,1,0:T(8,128)(2,1)}, u32[]{:S(2)}, u32[]{:S(2)}) async-start(bf16[128,6,2048]{2,1,0:T(8,128)(2,1)} %all_to_all.19), calls=%async_computation.1 | async-start | bytes 8388608 | tf_op jit(solution)/shard_map/all_to_all | solution.py:72
where the time goes:
time: 262 us; the launch traced here: 259 us
  blocking collectives  70.7 us (27%)
  waiting for transfers between devices  58.5 us (22%)
  matrix products  53.2 us (20%)
  local copies, waits for them, and re-layouts  51.6 us (20%)
  other arithmetic  16 us (6%)
  starting transfers between devices  8.84 us (3%)
    all_to_all x1, blocking collectives, body(): recv = lax.all_to_all(buf, 'ep', 0, 0, tiled=True)  70.7 us
    all_to_all x1, waiting for transfers between devices, body(): back = lax.all_to_all(e_out, 'ep', 0, 0, tiled=True)  58.5 us
    dot_general x3, matrix products, proj(): jnp.dot(xn, w, preferred_element_type=jnp.float32).astype(jnp.bfloat16)  22 us
    all_to_all x2, local copies, waits for them, and re-layouts, body(): back = lax.all_to_all(e_out, 'ep', 0, 0, tiled=True)  12.6 us
    all_to_all x2, local copies, waits for them, and re-layouts, body(): recv = lax.all_to_all(buf, 'ep', 0, 0, tiled=True)  12.6 us
    dot_general x1, matrix products, body(): jnp.einsum('gnf,gfd->gnd', u, w2, preferred_element_type=jnp.float32)  11 us
    dot_general x1, matrix products, body(): jnp.dot(o.reshape(t, heads * HEAD), wo, preferred_element_type=jnp.float32)  9.88 us
    all_to_all x1, starting transfers between devices, body(): back = lax.all_to_all(e_out, 'ep', 0, 0, tiled=True)  8.84 us
  transfers between devices with their start and end apart: 1, of which 1 were waited for; matrix products, arithmetic and copies ran while one was open for 0% of the time, Pallas kernels for 0%

commit v1 on v0

v1 whole, which is shorter than its diff:
```python
import functools

import jax
import jax.numpy as jnp
from jax import lax
from jax.experimental import pallas as pl
from jax.experimental.pallas import tpu as pltpu
from jax.sharding import PartitionSpec as P

EPS = 1e-6
HEAD = 128
LANES = 128
MESH = pl.DeviceIdType.MESH
NBUF = 3
CHUNKS = 8
COLS = 512


def torus_axes(n):
    if n == 128:
        return ((4, 32, 1), (4, 8, 4), (4, 2, 16), (2, 1, 64))
    axes, stride = [], 1
    while stride < n:
        axes.append((2, stride, stride))
        stride *= 2
    return tuple(axes)


def peer(n, me, i, sign):
    d = 0
    for size, stride, dig in torus_axes(n):
        own = (me // stride) % size
        off = (i // dig) % size
        d = d + ((own + sign * off + size) % size) * stride
    return d


def rms(xf, g):
    return (xf * lax.rsqrt(jnp.mean(xf * xf, axis=-1, keepdims=True) + EPS) * g).astype(jnp.bfloat16)


def dotf(a, b):
    return jnp.dot(a, b, preferred_element_type=jnp.float32)


def layer_kernel(n, cap, top,
                 x_hbm, idx_hbm, gate_ref, g1_hbm, g2_hbm, wq, wk, wv, wo, w1, w3, w2,
                 y_ref,
                 xv, idxv, g1v, g2v, bq, bk, bv, bo, e1, e3, e2,
                 xn, acc, hv, tokv, dstv, toks, dsts,
                 rows32, zt, send, recv, xs, esend, back, moe32,
                 in_sem, w_sem, e_sem, s_sem, out_ssem, out_rsem, ret_ssem, ret_rsem):
    t_len, d_model = xv.shape
    kb = d_model // LANES
    wid = wq.shape[1]
    cols = bq.shape[2]
    groups = wid // cols
    per = n // CHUNKS
    rows = per * cap
    me = lax.axis_index('ep')

    def weight_copies(g, slot):
        c = pl.ds(pl.multiple_of(g * cols, cols), cols)
        return [
            pltpu.make_async_copy(wq.at[:, c], bq.at[slot], w_sem.at[slot, 0]),
            pltpu.make_async_copy(wk.at[:, c], bk.at[slot], w_sem.at[slot, 1]),
            pltpu.make_async_copy(wv.at[:, c], bv.at[slot], w_sem.at[slot, 2]),
            pltpu.make_async_copy(wo.at[c, :], bo.at[slot], w_sem.at[slot, 3]),
        ]

    ins = [
        pltpu.make_async_copy(x_hbm, xv, in_sem.at[0]),
        pltpu.make_async_copy(idx_hbm, idxv, in_sem.at[1]),
        pltpu.make_async_copy(g1_hbm, g1v, in_sem.at[2]),
        pltpu.make_async_copy(g2_hbm, g2v, in_sem.at[3]),
    ]
    for cp in ins:
        cp.start()
    for g in range(min(NBUF, groups)):
        for cp in weight_copies(g, g):
            cp.start()
    experts = [
        pltpu.make_async_copy(w1, e1, e_sem.at[0]),
        pltpu.make_async_copy(w3, e3, e_sem.at[1]),
        pltpu.make_async_copy(w2, e2, e_sem.at[2]),
    ]

    barrier = pltpu.get_barrier_semaphore()

    def hello(i, carry):
        pl.semaphore_signal(barrier, inc=1, device_id={'ep': peer(n, me, i, 1)}, device_id_type=MESH)
        return carry

    lax.fori_loop(1, n, hello, 0)

    for cp in ins:
        cp.wait()
    exp = lax.broadcasted_iota(jnp.int32, (n, t_len), 0)
    member = jnp.zeros((n, t_len), jnp.float32)
    for j in range(top):
        member = member + (idxv[j:j + 1, :] == exp).astype(jnp.float32)
    before = lax.broadcasted_iota(jnp.int32, (t_len, t_len), 0) < lax.broadcasted_iota(jnp.int32, (t_len, t_len), 1)
    pos = dotf(member.astype(jnp.bfloat16), before.astype(jnp.bfloat16))
    off = jnp.zeros((n, t_len), jnp.int32)
    for size, stride, dig in torus_axes(n):
        own = (me // stride) % size
        off = off + (((exp // stride) % size + size - own) % size) * dig
    place = (off * cap).astype(jnp.float32) + pos
    for j in range(top):
        hit = jnp.where(idxv[j:j + 1, :] == exp, place, 0.0)
        dstv[j:j + 1, :] = jnp.clip(jnp.sum(hit, axis=0, keepdims=True).astype(jnp.int32), 0, n * cap - 1)
    tok = lax.broadcasted_iota(jnp.int32, (n, t_len), 1).astype(jnp.float32)
    for c in range(cap):
        hit = jnp.where((member > 0) & (pos == c), tok, 0.0)
        tokv[:, c:c + 1] = jnp.clip(jnp.sum(hit, axis=1, keepdims=True).astype(jnp.int32), 0, t_len - 1)
    tables = [
        pltpu.make_async_copy(tokv, toks, s_sem.at[0]),
        pltpu.make_async_copy(dstv, dsts, s_sem.at[1]),
    ]
    for cp in tables:
        cp.start()

    xn[...] = rms(xv[...].astype(jnp.float32), g1v[...])
    acc[...] = jnp.zeros_like(acc)
    keep = lax.broadcasted_iota(jnp.int32, (t_len, t_len), 0) >= lax.broadcasted_iota(jnp.int32, (t_len, t_len), 1)

    def group(g, carry):
        slot = g % NBUF
        for cp in weight_copies(g, slot):
            cp.wait()
        a = xn[...]
        q = dotf(a, bq[slot]).astype(jnp.bfloat16)
        k = dotf(a, bk[slot]).astype(jnp.bfloat16)
        v = dotf(a, bv[slot]).astype(jnp.bfloat16)
        outs = []
        for hd in range(cols // HEAD):
            c = slice(hd * HEAD, (hd + 1) * HEAD)
            sc = lax.dot_general(q[:, c], k[:, c], (((1,), (1,)), ((), ())),
                                 preferred_element_type=jnp.float32) * HEAD ** -0.5
            sc = jnp.where(keep, sc, -1e30)
            ex = jnp.exp(sc - jnp.max(sc, axis=-1, keepdims=True))
            p = (ex / jnp.sum(ex, axis=-1, keepdims=True)).astype(jnp.bfloat16)
            outs.append(dotf(p, v[:, c]).astype(jnp.bfloat16))
        o = jnp.concatenate(outs, axis=1)
        acc[...] += dotf(o, bo[slot])

        @pl.when(g + NBUF < groups)
        def _():
            for cp in weight_copies(g + NBUF, slot):
                cp.start()

        @pl.when(g + NBUF == groups)
        def _():
            for cp in experts:
                cp.start()

        return carry

    lax.fori_loop(0, groups, group, 0)

    h = (xv[...].astype(jnp.float32) + acc[...].astype(jnp.bfloat16).astype(jnp.float32)).astype(jnp.bfloat16)
    hv[...] = h
    z = rms(h.astype(jnp.float32), g2v[...]).astype(jnp.float32)
    for b in range(kb):
        rows32[:t_len, b, :] = z[:, b * LANES:(b + 1) * LANES]
    zt[...] = rows32[:t_len].astype(jnp.bfloat16)
    for cp in tables:
        cp.wait()

    pl.semaphore_wait(barrier, n - 1)
    for c in range(cap):
        recv[c] = zt[toks[me, c]]

    def out_copy(i):
        blk = pl.ds(i * cap, cap)
        return pltpu.make_async_remote_copy(
            src_ref=send.at[blk], dst_ref=recv.at[blk],
            send_sem=out_ssem, recv_sem=out_rsem.at[i // per],
            device_id={'ep': peer(n, me, i, 1)}, device_id_type=MESH)

    def fill(i):
        d = peer(n, me, i, 1)
        for c in range(cap):
            send[i * cap + c] = zt[toks[d, c]]

    fill(1)

    def dispatch(i, carry):
        fill(i)
        out_copy(i - 1).start()
        return carry

    lax.fori_loop(2, n, dispatch, 0)
    out_copy(n - 1).start()

    for cp in experts:
        cp.wait()
    other = peer(n, me, 1, 1)

    def got(first, count, dst, sem):
        blk = pl.ds(first, count)
        return pltpu.make_async_remote_copy(
            src_ref=send.at[blk], dst_ref=dst.at[blk], send_sem=out_ssem, recv_sem=sem,
            device_id={'ep': other}, device_id_type=MESH)

    def ret_copy(i):
        blk = pl.ds(i * cap, cap)
        return pltpu.make_async_remote_copy(
            src_ref=esend.at[blk], dst_ref=back.at[blk],
            send_sem=ret_ssem, recv_sem=ret_rsem,
            device_id={'ep': peer(n, me, i, -1)}, device_id_type=MESH)

    def chunk(ch, carry):
        @pl.when(ch == 0)
        def _():
            got(cap, rows - cap, recv, out_rsem.at[0]).wait_recv()

        @pl.when(ch > 0)
        def _():
            got(ch * rows, rows, recv, out_rsem.at[ch]).wait_recv()

        base = ch * rows
        rows32[:rows] = recv[pl.ds(base, rows)].astype(jnp.float32)
        for b in range(kb):
            xs[:, b * LANES:(b + 1) * LANES] = rows32[:rows, b, :].astype(jnp.bfloat16)
        r = xs[...]
        h1 = dotf(r, e1[...])
        h3 = dotf(r, e3[...])
        u = (jax.nn.silu(h1) * h3).astype(jnp.bfloat16)
        eo = dotf(u, e2[...])
        for b in range(kb):
            rows32[:rows, b, :] = eo[:, b * LANES:(b + 1) * LANES]
        esend[pl.ds(base, rows)] = rows32[:rows].astype(jnp.bfloat16)

        @pl.when(ch == 0)
        def _():
            back[:cap] = esend[:cap]

        def give(b, c2):
            ret_copy(ch * per + b).start()
            return c2

        lax.fori_loop(jnp.where(ch == 0, 1, 0), per, give, 0)
        return carry

    lax.fori_loop(0, CHUNKS, chunk, 0)

    whole = pl.ds(cap, (n - 1) * cap)
    tail = pltpu.make_async_remote_copy(
        src_ref=esend.at[whole], dst_ref=back.at[whole], send_sem=ret_ssem, recv_sem=ret_rsem,
        device_id={'ep': other}, device_id_type=MESH)
    tail.wait_recv()

    def combine(t, carry):
        total = jnp.zeros((kb, LANES), jnp.float32)
        for j in range(top):
            total = total + back[dsts[j, t]].astype(jnp.float32) * gate_ref[j, t]
        moe32[t] = total
        return carry

    lax.fori_loop(0, t_len, combine, 0)
    for b in range(kb):
        c = slice(b * LANES, (b + 1) * LANES)
        y_ref[:, c] = (hv[:, c].astype(jnp.float32) + moe32[:, b, :]).astype(jnp.bfloat16)

    pltpu.make_async_remote_copy(
        src_ref=send.at[whole], dst_ref=recv.at[whole], send_sem=out_ssem, recv_sem=ret_rsem,
        device_id={'ep': other}, device_id_type=MESH).wait_send()
    tail.wait_send()


def layer(n, x, idx, gates, g1, g2, wq, wk, wv, wo, w1, w3, w2):
    t_len, d = x.shape
    top = idx.shape[0]
    avg = top * t_len // n
    cap = avg + avg // 2
    cols = min(COLS, wq.shape[1])
    kb = d // LANES
    ff = w1.shape[1]
    per = n // CHUNKS
    rows = per * cap
    bf, f32, i32 = jnp.bfloat16, jnp.float32, jnp.int32
    anyspec = pl.BlockSpec(memory_space=pl.ANY)
    V, DMA = pltpu.VMEM, pltpu.SemaphoreType.DMA
    return pl.pallas_call(
        functools.partial(layer_kernel, n, cap, top),
        out_shape=jax.ShapeDtypeStruct((t_len, d), bf),
        in_specs=[anyspec, anyspec, pl.BlockSpec(memory_space=pltpu.SMEM)] + [anyspec] * 9,
        out_specs=pl.BlockSpec(memory_space=pltpu.VMEM),
        scratch_shapes=[
            V((t_len, d), bf), V((top, t_len), i32), V((1, d), f32), V((1, d), f32),
            V((NBUF, d, cols), bf), V((NBUF, d, cols), bf), V((NBUF, d, cols), bf), V((NBUF, cols, d), bf),
            V((d, ff), bf), V((d, ff), bf), V((ff, d), bf),
            V((t_len, d), bf), V((t_len, d), f32), V((t_len, d), bf),
            V((n, cap), i32), V((top, t_len), i32), pltpu.SMEM((n, cap), i32), pltpu.SMEM((top, t_len), i32),
            V((max(rows, t_len), kb, LANES), f32), V((t_len, kb, LANES), bf),
            V((n * cap, kb, LANES), bf), V((n * cap, kb, LANES), bf), V((rows, d), bf),
            V((n * cap, kb, LANES), bf), V((n * cap, kb, LANES), bf), V((t_len, kb, LANES), f32),
            DMA((4,)), DMA((NBUF, 4)), DMA((3,)), DMA((2,)), DMA, DMA((CHUNKS,)), DMA, DMA,
        ],
        compiler_params=pltpu.CompilerParams(
            collective_id=0, has_side_effects=True, vmem_limit_bytes=67043328),
        name='layer',
    )(x, idx, gates, g1, g2, wq, wk, wv, wo, w1, w3, w2)


def solution(mesh):
    n = mesh.shape['ep']
    tok = P(('dp', 'ep'))
    rep = P()
    exs = P('ep')

    def body(x, idx, gates, g1, wq, wk, wv, wo, g2, w1, w3, w2):
        d = x.shape[-1]
        y = layer(n, x[0], idx[0].T, gates[0].T, g1.reshape(1, d), g2.reshape(1, d),
                  wq, wk, wv, wo, w1[0], w3[0], w2[0])
        return y[None]

    return jax.shard_map(body, mesh=mesh, in_specs=(tok, tok, tok, rep, rep, rep, rep, rep, rep, exs, exs, exs), out_specs=tok, check_vma=False)
```

time: 262 us -> 126 us (0.48)
  the two profiles are of different devices: /device:TPU:1 before, /device:TPU:3 now
where the time goes in v1:
time: 126 us
  Pallas kernels  124 us (98%)
  local copies, waits for them, and re-layouts  1.67 us (1%)
    pallas_call x1, Pallas kernels, layer(): pl.pallas_call(functools.partial(layer_kernel, n, cap, top), out_shape=ja...  124 us

profile of v1, /device:TPU:3, one launch (start us, length us, event | category | flops | bytes accessed | tf_op | source)
XLA Modules:
  0.0 126.0 jit_solution(18251141180811396210)
XLA Ops:
  0.0 124.3 %layer.1 = bf16[64,2048]{1,0:T(8,128)(2,1)} custom-call(bf16[64,2048]{1,0:T(8,128)(2,1)} %bitcast.17, s32[8,64]{1,0:T(8,128)} %bitcast.20, f32[8,64]{1,0:T(8,128)} %bitcast.21, f32[1,2048]{1,0:T(1,128)} %bitcast.18, f32[1,2048]{1,0:T(1,128)} %bitcast.19, bf16[2048,4096]{1,0:T(8,128)(2,1)} %wq.1, bf16[2048,4096]{1,0:T(8,128)(2,1)} %wk.1, ...), custom_call_target="tpu_custom_call" | custom-call | tf_op jit(solution)/shard_map/layer/pallas_call | solution.py:285
  124.3 1.7 %copy.14 = bf16[1,64,2048]{2,1,0:T(8,128)(2,1)} copy(bf16[1,64,2048]{2,1,0:T(8,128)(2,1)} %bitcast.16) | data formatting | bytes 524288

commit v2 on v1

--- a/solution.py
+++ b/solution.py
@@ -18,19 +18,37 @@
 
 def torus_axes(n):
     if n == 128:
-        return ((4, 32, 1), (4, 8, 4), (4, 2, 16), (2, 1, 64))
+        return ((4, 32), (4, 8), (4, 2), (2, 1))
     axes, stride = [], 1
     while stride < n:
-        axes.append((2, stride, stride))
+        axes.append((2, stride))
         stride *= 2
     return tuple(axes)
 
 
+def steps(n, i):
+    axes = torus_axes(n)
+    out, div = [], 1
+    for size, _ in axes:
+        out.append((i // div + (i if div > 1 else 0)) % size)
+        div *= size
+    return out
+
+
+def number(n, deltas):
+    axes = torus_axes(n)
+    i, div = deltas[0], axes[0][0]
+    for (size, _), d in zip(axes[1:], deltas[1:]):
+        low = i
+        i = i + ((d - low % size + size) % size) * div
+        div *= size
+    return i
+
+
 def peer(n, me, i, sign):
     d = 0
-    for size, stride, dig in torus_axes(n):
+    for (size, stride), off in zip(torus_axes(n), steps(n, i)):
         own = (me // stride) % size
-        off = (i // dig) % size
         d = d + ((own + sign * off + size) % size) * stride
     return d
 
@@ -44,23 +62,26 @@
 
 
 def layer_kernel(n, cap, top,
-                 x_hbm, idx_hbm, gate_ref, g1_hbm, g2_hbm, wq, wk, wv, wo, w1, w3, w2,
+                 x_hbm, xp_hbm, idx_hbm, gate_ref, g1_hbm, g2_hbm, wq, wk, wv, wo, w1, w3, w2,
                  y_ref,
                  xv, idxv, g1v, g2v, bq, bk, bv, bo, e1, e3, e2,
-                 xn, acc, hv, tokv, dstv, toks, dsts,
+                 xn, acc, part, hv, tokv, dstv, toks, dsts,
                  rows32, zt, send, recv, xs, esend, back, moe32,
-                 in_sem, w_sem, e_sem, s_sem, out_ssem, out_rsem, ret_ssem, ret_rsem):
-    t_len, d_model = xv.shape
+                 in_sem, w_sem, e_sem, s_sem, p_ssem, p_rsem, out_ssem, out_rsem, ret_ssem, ret_rsem):
+    t2, d_model = xv.shape
+    t_len = t2 // 2
     kb = d_model // LANES
     wid = wq.shape[1]
     cols = bq.shape[2]
-    groups = wid // cols
+    groups = wid // 2 // cols
     per = n // CHUNKS
     rows = per * cap
     me = lax.axis_index('ep')
+    core = me % 2
+    mate = me + 1 - 2 * core
 
     def weight_copies(g, slot):
-        c = pl.ds(pl.multiple_of(g * cols, cols), cols)
+        c = pl.ds(pl.multiple_of((core * groups + g) * cols, cols), cols)
         return [
             pltpu.make_async_copy(wq.at[:, c], bq.at[slot], w_sem.at[slot, 0]),
             pltpu.make_async_copy(wk.at[:, c], bk.at[slot], w_sem.at[slot, 1]),
@@ -69,7 +90,8 @@
         ]
 
     ins = [
-        pltpu.make_async_copy(x_hbm, xv, in_sem.at[0]),
+        pltpu.make_async_copy(x_hbm, xv.at[:t_len], in_sem.at[0]),
+        pltpu.make_async_copy(xp_hbm, xv.at[t_len:], in_sem.at[4]),
         pltpu.make_async_copy(idx_hbm, idxv, in_sem.at[1]),
         pltpu.make_async_copy(g1_hbm, g1v, in_sem.at[2]),
         pltpu.make_async_copy(g2_hbm, g2v, in_sem.at[3]),
@@ -101,10 +123,8 @@
         member = member + (idxv[j:j + 1, :] == exp).astype(jnp.float32)
     before = lax.broadcasted_iota(jnp.int32, (t_len, t_len), 0) < lax.broadcasted_iota(jnp.int32, (t_len, t_len), 1)
     pos = dotf(member.astype(jnp.bfloat16), before.astype(jnp.bfloat16))
-    off = jnp.zeros((n, t_len), jnp.int32)
-    for size, stride, dig in torus_axes(n):
-        own = (me // stride) % size
-        off = off + (((exp // stride) % size + size - own) % size) * dig
+    off = number(n, [((exp // stride) % size + size - (me // stride) % size) % size
+                     for size, stride in torus_axes(n)])
     place = (off * cap).astype(jnp.float32) + pos
     for j in range(top):
         hit = jnp.where(idxv[j:j + 1, :] == exp, place, 0.0)
@@ -122,7 +142,9 @@
 
     xn[...] = rms(xv[...].astype(jnp.float32), g1v[...])
     acc[...] = jnp.zeros_like(acc)
-    keep = lax.broadcasted_iota(jnp.int32, (t_len, t_len), 0) >= lax.broadcasted_iota(jnp.int32, (t_len, t_len), 1)
+    row = lax.broadcasted_iota(jnp.int32, (t2, t2), 0)
+    col = lax.broadcasted_iota(jnp.int32, (t2, t2), 1)
+    keep = (row >= col) & (row // t_len == col // t_len)
 
     def group(g, carry):
         slot = g % NBUF
@@ -158,7 +180,14 @@
 
     lax.fori_loop(0, groups, group, 0)
 
-    h = (xv[...].astype(jnp.float32) + acc[...].astype(jnp.bfloat16).astype(jnp.float32)).astype(jnp.bfloat16)
+    pl.semaphore_wait(barrier, n - 1)
+    swap = pltpu.make_async_remote_copy(
+        src_ref=acc.at[t_len:], dst_ref=part, send_sem=p_ssem, recv_sem=p_rsem,
+        device_id={'ep': mate}, device_id_type=MESH)
+    swap.start()
+    swap.wait()
+    att = (acc[:t_len] + part[...]).astype(jnp.bfloat16)
+    h = (xv[:t_len].astype(jnp.float32) + att.astype(jnp.float32)).astype(jnp.bfloat16)
     hv[...] = h
     z = rms(h.astype(jnp.float32), g2v[...]).astype(jnp.float32)
     for b in range(kb):
@@ -167,7 +196,6 @@
     for cp in tables:
         cp.wait()
 
-    pl.semaphore_wait(barrier, n - 1)
     for c in range(cap):
         recv[c] = zt[toks[me, c]]
 
@@ -269,12 +297,12 @@
     tail.wait_send()
 
 
-def layer(n, x, idx, gates, g1, g2, wq, wk, wv, wo, w1, w3, w2):
+def layer(n, x, xp, idx, gates, g1, g2, wq, wk, wv, wo, w1, w3, w2):
     t_len, d = x.shape
     top = idx.shape[0]
     avg = top * t_len // n
     cap = avg + avg // 2
-    cols = min(COLS, wq.shape[1])
+    cols = min(COLS, wq.shape[1] // 2)
     kb = d // LANES
     ff = w1.shape[1]
     per = n // CHUNKS
@@ -285,23 +313,23 @@
     return pl.pallas_call(
         functools.partial(layer_kernel, n, cap, top),
         out_shape=jax.ShapeDtypeStruct((t_len, d), bf),
-        in_specs=[anyspec, anyspec, pl.BlockSpec(memory_space=pltpu.SMEM)] + [anyspec] * 9,
+        in_specs=[anyspec, anyspec, anyspec, pl.BlockSpec(memory_space=pltpu.SMEM)] + [anyspec] * 9,
         out_specs=pl.BlockSpec(memory_space=pltpu.VMEM),
         scratch_shapes=[
-            V((t_len, d), bf), V((top, t_len), i32), V((1, d), f32), V((1, d), f32),
+            V((2 * t_len, d), bf), V((top, t_len), i32), V((1, d), f32), V((1, d), f32),
             V((NBUF, d, cols), bf), V((NBUF, d, cols), bf), V((NBUF, d, cols), bf), V((NBUF, cols, d), bf),
             V((d, ff), bf), V((d, ff), bf), V((ff, d), bf),
-            V((t_len, d), bf), V((t_len, d), f32), V((t_len, d), bf),
+            V((2 * t_len, d), bf), V((2 * t_len, d), f32), V((t_len, d), f32), V((t_len, d), bf),
             V((n, cap), i32), V((top, t_len), i32), pltpu.SMEM((n, cap), i32), pltpu.SMEM((top, t_len), i32),
             V((max(rows, t_len), kb, LANES), f32), V((t_len, kb, LANES), bf),
             V((n * cap, kb, LANES), bf), V((n * cap, kb, LANES), bf), V((rows, d), bf),
             V((n * cap, kb, LANES), bf), V((n * cap, kb, LANES), bf), V((t_len, kb, LANES), f32),
-            DMA((4,)), DMA((NBUF, 4)), DMA((3,)), DMA((2,)), DMA, DMA((CHUNKS,)), DMA, DMA,
+            DMA((5,)), DMA((NBUF, 4)), DMA((3,)), DMA((2,)), DMA, DMA, DMA, DMA((CHUNKS,)), DMA, DMA,
         ],
         compiler_params=pltpu.CompilerParams(
             collective_id=0, has_side_effects=True, vmem_limit_bytes=67043328),
         name='layer',
-    )(x, idx, gates, g1, g2, wq, wk, wv, wo, w1, w3, w2)
+    )(x, xp, idx, gates, g1, g2, wq, wk, wv, wo, w1, w3, w2)
 
 
 def solution(mesh):
@@ -312,7 +340,8 @@
 
     def body(x, idx, gates, g1, wq, wk, wv, wo, g2, w1, w3, w2):
         d = x.shape[-1]
-        y = layer(n, x[0], idx[0].T, gates[0].T, g1.reshape(1, d), g2.reshape(1, d),
+        xp = lax.ppermute(x[0], 'ep', [(i, i ^ 1) for i in range(n)])
+        y = layer(n, x[0], xp, idx[0].T, gates[0].T, g1.reshape(1, d), g2.reshape(1, d),
                   wq, wk, wv, wo, w1[0], w3[0], w2[0])
         return y[None]
 

time: 126 us -> 115 us (0.913)
  the two profiles are of different devices: /device:TPU:3 before, /device:TPU:1 now
where the time goes in v2:
time: 115 us; the launch traced here: 114 us
  Pallas kernels  110 us (96%)
  local copies, waits for them, and re-layouts  1.67 us (1%)
  starting transfers between devices  1.36 us (1%)
  waiting for transfers between devices  1.16 us (1%)
    pallas_call x1, Pallas kernels, layer(): pl.pallas_call(functools.partial(layer_kernel, n, cap, top), out_shape=ja...  110 us
  transfers between devices with their start and end apart: 1, of which 1 were waited for; matrix products, arithmetic and copies ran while one was open for 0% of the time, Pallas kernels for 0%

profile of v2, /device:TPU:1, one launch (start us, length us, event | category | flops | bytes accessed | tf_op | source)
XLA Modules:
  0.0 114.4 jit_solution(4183965369034734664)
XLA Ops:
  0.0 1.4 %collective-permute-start = (bf16[64,2048]{1,0:T(8,128)(2,1)}, bf16[64,2048]{1,0:T(8,128)(2,1)}, u32[]{:S(2)}, u32[]{:S(2)}) collective-permute-start(bf16[64,2048]{1,0:T(8,128)(2,1)} %bitcast.17), channel_id=1, source_target_pairs={{0,1},{1,0},{2,3},{3,2},{4,5},{5,4},{6,7},{7,6},{8,9},{9,8},{10,11... | collective-permute-start | bytes 786440 | tf_op jit(solution)/shard_map/ppermute | solution.py:343
  1.4 1.2 %collective-permute-done.xp_hbm = bf16[64,2048]{1,0:T(8,128)(2,1)} collective-permute-done((bf16[64,2048]{1,0:T(8,128)(2,1)}, bf16[64,2048]{1,0:T(8,128)(2,1)}, u32[]{:S(2)}, u32[]{:S(2)}) %collective-permute-start) | collective-permute-done | bytes 262176 | tf_op jit(solution)/shard_map/ppermute | solution.py:343
  2.5 110.2 %layer.1 = bf16[64,2048]{1,0:T(8,128)(2,1)} custom-call(bf16[64,2048]{1,0:T(8,128)(2,1)} %bitcast.18, bf16[64,2048]{1,0:T(8,128)(2,1)} %collective-permute-done.xp_hbm, s32[8,64]{1,0:T(8,128)} %bitcast.21, f32[8,64]{1,0:T(8,128)} %bitcast.22, f32[1,2048]{1,0:T(1,128)} %bitcast.19, f32[1,2048]{1,0:T(1,128)} %bitcast.20, bf16[2048,4096]{1,0:T(8,128)(2,1)} %wq.1, ...), custom_call_target="tpu_custom_call" | custom-call | tf_op jit(solution)/shard_map/layer/pallas_call | solution.py:313
  112.7 1.7 %copy.14 = bf16[1,64,2048]{2,1,0:T(8,128)(2,1)} copy(bf16[1,64,2048]{2,1,0:T(8,128)(2,1)} %bitcast.16) | data formatting | bytes 524288
Async XLA Ops:
  0.0 2.5 %collective-permute-start = (bf16[64,2048]{1,0:T(8,128)(2,1)}, bf16[64,2048]{1,0:T(8,128)(2,1)}, u32[]{:S(2)}, u32[]{:S(2)}) collective-permute-start(bf16[64,2048]{1,0:T(8,128)(2,1)} %bitcast.17), channel_id=1, source_target_pairs={{0,1},{1,0},{2,3},{3,2},{4,5},{5,4},{6,7},{7,6},{8,9},{9,8},{10,11... | collective-permute-start | bytes 786440 | tf_op jit(solution)/shard_map/ppermute | solution.py:343

commit v3 on v2

--- a/solution.py
+++ b/solution.py
@@ -11,8 +11,9 @@
 HEAD = 128
 LANES = 128
 MESH = pl.DeviceIdType.MESH
-NBUF = 3
-CHUNKS = 8
+NBUF = 4
+PAIR = 2
+PARTS = 2
 COLS = 512
 
 
@@ -26,15 +27,6 @@
     return tuple(axes)
 
 
-def steps(n, i):
-    axes = torus_axes(n)
-    out, div = [], 1
-    for size, _ in axes:
-        out.append((i // div + (i if div > 1 else 0)) % size)
-        div *= size
-    return out
-
-
 def number(n, deltas):
     axes = torus_axes(n)
     i, div = deltas[0], axes[0][0]
@@ -45,11 +37,13 @@
     return i
 
 
-def peer(n, me, i, sign):
-    d = 0
-    for (size, stride), off in zip(torus_axes(n), steps(n, i)):
-        own = (me // stride) % size
-        d = d + ((own + sign * off + size) % size) * stride
+def peer(n, own, q, a, sign):
+    axes = torus_axes(n)
+    d, div = 0, 1
+    for k, (size, stride) in enumerate(axes):
+        step = a if k == 0 else lax.rem(lax.div(q, div) + a, size)
+        d = d + lax.rem(own[k] + sign * step + size, size) * stride
+        div *= size if k else 1
     return d
 
 
@@ -63,9 +57,9 @@
 
 def layer_kernel(n, cap, top,
                  x_hbm, xp_hbm, idx_hbm, gate_ref, g1_hbm, g2_hbm, wq, wk, wv, wo, w1, w3, w2,
-                 y_ref,
+                 hv, moe_ref,
                  xv, idxv, g1v, g2v, bq, bk, bv, bo, e1, e3, e2,
-                 xn, acc, part, hv, tokv, dstv, toks, dsts,
+                 xn, acc, part, tokv, dstv, toks, dsts,
                  rows32, zt, send, recv, xs, esend, back, moe32,
                  in_sem, w_sem, e_sem, s_sem, p_ssem, p_rsem, out_ssem, out_rsem, ret_ssem, ret_rsem):
     t2, d_model = xv.shape
@@ -74,10 +68,13 @@
     wid = wq.shape[1]
     cols = bq.shape[2]
     groups = wid // 2 // cols
-    per = n // CHUNKS
-    rows = per * cap
+    passes = cap // PAIR
+    per = n // PARTS
+    rows = per * PAIR
+    first = torus_axes(n)[0][0]
     me = lax.axis_index('ep')
-    core = me % 2
+    own = [lax.rem(lax.div(me, stride), size) for size, stride in torus_axes(n)]
+    core = lax.rem(me, 2)
     mate = me + 1 - 2 * core
 
     def weight_copies(g, slot):
@@ -109,11 +106,12 @@
 
     barrier = pltpu.get_barrier_semaphore()
 
-    def hello(i, carry):
-        pl.semaphore_signal(barrier, inc=1, device_id={'ep': peer(n, me, i, 1)}, device_id_type=MESH)
+    def hello(j, carry):
+        pl.semaphore_signal(barrier, inc=1, device_id={'ep': j}, device_id_type=MESH)
         return carry
 
-    lax.fori_loop(1, n, hello, 0)
+    lax.fori_loop(me + 1, n, hello, 0)
+    lax.fori_loop(0, me, hello, 0)
 
     for cp in ins:
         cp.wait()
@@ -125,7 +123,8 @@
     pos = dotf(member.astype(jnp.bfloat16), before.astype(jnp.bfloat16))
     off = number(n, [((exp // stride) % size + size - (me // stride) % size) % size
                      for size, stride in torus_axes(n)])
-    place = (off * cap).astype(jnp.float32) + pos
+    nth = pos.astype(jnp.int32)
+    place = (((nth // PAIR) * n + off) * PAIR + nth % PAIR).astype(jnp.float32)
     for j in range(top):
         hit = jnp.where(idxv[j:j + 1, :] == exp, place, 0.0)
         dstv[j:j + 1, :] = jnp.clip(jnp.sum(hit, axis=0, keepdims=True).astype(jnp.int32), 0, n * cap - 1)
@@ -171,7 +170,7 @@
             for cp in weight_copies(g + NBUF, slot):
                 cp.start()
 
-        @pl.when(g + NBUF == groups)
+        @pl.when(g == max(groups - 2, 0))
         def _():
             for cp in experts:
                 cp.start()
@@ -196,58 +195,75 @@
     for cp in tables:
         cp.wait()
 
-    for c in range(cap):
-        recv[c] = zt[toks[me, c]]
-
-    def out_copy(i):
-        blk = pl.ds(i * cap, cap)
+    for p in range(passes):
+        for c in range(PAIR):
+            recv[p * n * PAIR + c] = zt[toks[me, p * PAIR + c]]
+
+    def block(p, i):
+        return pl.ds((p * n + i) * PAIR, PAIR)
+
+    def fill(p, q, a):
+        d = peer(n, own, q, a, 1)
+        for c in range(PAIR):
+            send[(p * n + first * q + a) * PAIR + c] = zt[toks[d, p * PAIR + c]]
+
+    def out_copy(p, q, a):
+        i = first * q + a
         return pltpu.make_async_remote_copy(
-            src_ref=send.at[blk], dst_ref=recv.at[blk],
-            send_sem=out_ssem, recv_sem=out_rsem.at[i // per],
-            device_id={'ep': peer(n, me, i, 1)}, device_id_type=MESH)
-
-    def fill(i):
-        d = peer(n, me, i, 1)
-        for c in range(cap):
-            send[i * cap + c] = zt[toks[d, c]]
-
-    fill(1)
-
-    def dispatch(i, carry):
-        fill(i)
-        out_copy(i - 1).start()
-        return carry
-
-    lax.fori_loop(2, n, dispatch, 0)
-    out_copy(n - 1).start()
+            src_ref=send.at[block(p, i)], dst_ref=recv.at[block(p, i)],
+            send_sem=out_ssem.at[p], recv_sem=out_rsem.at[p * PARTS + lax.div(i, per)],
+            device_id={'ep': peer(n, own, q, a, 1)}, device_id_type=MESH)
+
+    quads = n // first
+    for p in range(passes):
+        for a in range(first):
+            fill(p, 0, a)
+
+        def dispatch(q, carry):
+            for a in range(first):
+                fill(p, q, a)
+            for a in range(first):
+                if a == 0:
+                    @pl.when(q > 1)
+                    def _():
+                        out_copy(p, q - 1, a).start()
+                else:
+                    out_copy(p, q - 1, a).start()
+            return carry
+
+        lax.fori_loop(1, quads, dispatch, 0)
+        for a in range(first):
+            out_copy(p, quads - 1, a).start()
 
     for cp in experts:
         cp.wait()
-    other = peer(n, me, 1, 1)
-
-    def got(first, count, dst, sem):
-        blk = pl.ds(first, count)
+
+    def span(lo, count, src, dst, ssem, rsem):
+        blk = pl.ds(lo, count)
         return pltpu.make_async_remote_copy(
-            src_ref=send.at[blk], dst_ref=dst.at[blk], send_sem=out_ssem, recv_sem=sem,
-            device_id={'ep': other}, device_id_type=MESH)
-
-    def ret_copy(i):
-        blk = pl.ds(i * cap, cap)
+            src_ref=src.at[blk], dst_ref=dst.at[blk], send_sem=ssem, recv_sem=rsem,
+            device_id={'ep': mate}, device_id_type=MESH)
+
+    def ret_copy(p, q, a):
+        i = first * q + a
         return pltpu.make_async_remote_copy(
-            src_ref=esend.at[blk], dst_ref=back.at[blk],
-            send_sem=ret_ssem, recv_sem=ret_rsem,
-            device_id={'ep': peer(n, me, i, -1)}, device_id_type=MESH)
+            src_ref=esend.at[block(p, i)], dst_ref=back.at[block(p, i)],
+            send_sem=ret_ssem.at[p], recv_sem=ret_rsem.at[p],
+            device_id={'ep': peer(n, own, q, a, -1)}, device_id_type=MESH)
 
     def chunk(ch, carry):
-        @pl.when(ch == 0)
-        def _():
-            got(cap, rows - cap, recv, out_rsem.at[0]).wait_recv()
-
-        @pl.when(ch > 0)
-        def _():
-            got(ch * rows, rows, recv, out_rsem.at[ch]).wait_recv()
-
+        p = lax.div(ch, PARTS)
+        half = lax.rem(ch, PARTS)
         base = ch * rows
+
+        @pl.when(half == 0)
+        def _():
+            span(base + PAIR, rows - PAIR, send, recv, out_ssem.at[0], out_rsem.at[ch]).wait_recv()
+
+        @pl.when(half > 0)
+        def _():
+            span(base, rows, send, recv, out_ssem.at[0], out_rsem.at[ch]).wait_recv()
+
         rows32[:rows] = recv[pl.ds(base, rows)].astype(jnp.float32)
         for b in range(kb):
             xs[:, b * LANES:(b + 1) * LANES] = rows32[:rows, b, :].astype(jnp.bfloat16)
@@ -260,24 +276,31 @@
             rows32[:rows, b, :] = eo[:, b * LANES:(b + 1) * LANES]
         esend[pl.ds(base, rows)] = rows32[:rows].astype(jnp.bfloat16)
 
-        @pl.when(ch == 0)
-        def _():
-            back[:cap] = esend[:cap]
-
-        def give(b, c2):
-            ret_copy(ch * per + b).start()
+        @pl.when(half == 0)
+        def _():
+            back[pl.ds(base, PAIR)] = esend[pl.ds(base, PAIR)]
+
+        def give(k, c2):
+            q = half * (quads // PARTS) + k
+            for a in range(first):
+                if a == 0:
+                    @pl.when(q > 0)
+                    def _():
+                        ret_copy(p, q, a).start()
+                else:
+                    ret_copy(p, q, a).start()
             return c2
 
-        lax.fori_loop(jnp.where(ch == 0, 1, 0), per, give, 0)
+        lax.fori_loop(0, quads // PARTS, give, 0)
         return carry
 
-    lax.fori_loop(0, CHUNKS, chunk, 0)
-
-    whole = pl.ds(cap, (n - 1) * cap)
-    tail = pltpu.make_async_remote_copy(
-        src_ref=esend.at[whole], dst_ref=back.at[whole], send_sem=ret_ssem, recv_sem=ret_rsem,
-        device_id={'ep': other}, device_id_type=MESH)
-    tail.wait_recv()
+    lax.fori_loop(0, passes * PARTS, chunk, 0)
+
+    def full(p, src, dst, ssem, rsem):
+        return span((p * n + 1) * PAIR, (n - 1) * PAIR, src, dst, ssem, rsem)
+
+    for p in range(passes):
+        full(p, esend, back, ret_ssem.at[p], ret_rsem.at[p]).wait_recv()
 
     def combine(t, carry):
         total = jnp.zeros((kb, LANES), jnp.float32)
@@ -288,13 +311,11 @@
 
     lax.fori_loop(0, t_len, combine, 0)
     for b in range(kb):
-        c = slice(b * LANES, (b + 1) * LANES)
-        y_ref[:, c] = (hv[:, c].astype(jnp.float32) + moe32[:, b, :]).astype(jnp.bfloat16)
-
-    pltpu.make_async_remote_copy(
-        src_ref=send.at[whole], dst_ref=recv.at[whole], send_sem=out_ssem, recv_sem=ret_rsem,
-        device_id={'ep': other}, device_id_type=MESH).wait_send()
-    tail.wait_send()
+        moe_ref[:, b * LANES:(b + 1) * LANES] = moe32[:, b, :]
+
+    for p in range(passes):
+        full(p, send, recv, out_ssem.at[p], out_rsem.at[0]).wait_send()
+        full(p, esend, back, ret_ssem.at[p], ret_rsem.at[p]).wait_send()
 
 
 def layer(n, x, xp, idx, gates, g1, g2, wq, wk, wv, wo, w1, w3, w2):
@@ -305,26 +326,27 @@
     cols = min(COLS, wq.shape[1] // 2)
     kb = d // LANES
     ff = w1.shape[1]
-    per = n // CHUNKS
-    rows = per * cap
+    passes = cap // PAIR
+    rows = n // PARTS * PAIR
     bf, f32, i32 = jnp.bfloat16, jnp.float32, jnp.int32
     anyspec = pl.BlockSpec(memory_space=pl.ANY)
     V, DMA = pltpu.VMEM, pltpu.SemaphoreType.DMA
     return pl.pallas_call(
         functools.partial(layer_kernel, n, cap, top),
-        out_shape=jax.ShapeDtypeStruct((t_len, d), bf),
+        out_shape=(jax.ShapeDtypeStruct((t_len, d), bf), jax.ShapeDtypeStruct((t_len, d), f32)),
         in_specs=[anyspec, anyspec, anyspec, pl.BlockSpec(memory_space=pltpu.SMEM)] + [anyspec] * 9,
-        out_specs=pl.BlockSpec(memory_space=pltpu.VMEM),
+        out_specs=(pl.BlockSpec(memory_space=pltpu.VMEM), pl.BlockSpec(memory_space=pltpu.VMEM)),
         scratch_shapes=[
             V((2 * t_len, d), bf), V((top, t_len), i32), V((1, d), f32), V((1, d), f32),
             V((NBUF, d, cols), bf), V((NBUF, d, cols), bf), V((NBUF, d, cols), bf), V((NBUF, cols, d), bf),
             V((d, ff), bf), V((d, ff), bf), V((ff, d), bf),
-            V((2 * t_len, d), bf), V((2 * t_len, d), f32), V((t_len, d), f32), V((t_len, d), bf),
+            V((2 * t_len, d), bf), V((2 * t_len, d), f32), V((t_len, d), f32),
             V((n, cap), i32), V((top, t_len), i32), pltpu.SMEM((n, cap), i32), pltpu.SMEM((top, t_len), i32),
             V((max(rows, t_len), kb, LANES), f32), V((t_len, kb, LANES), bf),
             V((n * cap, kb, LANES), bf), V((n * cap, kb, LANES), bf), V((rows, d), bf),
             V((n * cap, kb, LANES), bf), V((n * cap, kb, LANES), bf), V((t_len, kb, LANES), f32),
-            DMA((5,)), DMA((NBUF, 4)), DMA((3,)), DMA((2,)), DMA, DMA, DMA, DMA((CHUNKS,)), DMA, DMA,
+            DMA((5,)), DMA((NBUF, 4)), DMA((3,)), DMA((2,)), DMA, DMA,
+            DMA((passes,)), DMA((passes * PARTS,)), DMA((passes,)), DMA((passes,)),
         ],
         compiler_params=pltpu.CompilerParams(
             collective_id=0, has_side_effects=True, vmem_limit_bytes=67043328),
@@ -341,8 +363,8 @@
     def body(x, idx, gates, g1, wq, wk, wv, wo, g2, w1, w3, w2):
         d = x.shape[-1]
         xp = lax.ppermute(x[0], 'ep', [(i, i ^ 1) for i in range(n)])
-        y = layer(n, x[0], xp, idx[0].T, gates[0].T, g1.reshape(1, d), g2.reshape(1, d),
+        h, moe = layer(n, x[0], xp, idx[0].T, gates[0].T, g1.reshape(1, d), g2.reshape(1, d),
                   wq, wk, wv, wo, w1[0], w3[0], w2[0])
-        return y[None]
+        return (h.astype(jnp.float32) + moe).astype(jnp.bfloat16)[None]
 
     return jax.shard_map(body, mesh=mesh, in_specs=(tok, tok, tok, rep, rep, rep, rep, rep, rep, exs, exs, exs), out_specs=tok, check_vma=False)

time: 115 us -> 109 us (0.948)
  Pallas kernels: 110 us -> 104 us
  other arithmetic: 0 us -> 1.86 us
  local copies, waits for them, and re-layouts: 1.67 us -> 0 us
    pallas_call x1, Pallas kernels: 110 us -> 104 us  [layer(): pl.pallas_call(functools.partial(layer_kernel, n, cap, top), out_shape=(j...]
    broadcast_in_dim x0 -> x1, other arithmetic: none -> 1.86 us  [body(): return (h.astype(jnp.float32) + moe).astype(jnp.bfloat16)[None]]
    unnamed x1 -> x0, local copies, waits for them, and re-layouts: 1.67 us -> none
where the time goes in v3:
time: 109 us
  Pallas kernels  104 us (95%)
  other arithmetic  1.86 us (2%)
  starting transfers between devices  1.36 us (1%)
  waiting for transfers between devices  1.16 us (1%)
    pallas_call x1, Pallas kernels, layer(): pl.pallas_call(functools.partial(layer_kernel, n, cap, top), out_shape=(j...  104 us
  transfers between devices with their start and end apart: 1, of which 1 were waited for; matrix products, arithmetic and copies ran while one was open for 0% of the time, Pallas kernels for 0%

profile of v3, /device:TPU:1, one launch (start us, length us, event | category | flops | bytes accessed | tf_op | source)
XLA Modules:
  0.0 108.6 jit_solution(5172945630761302514)
XLA Ops:
  0.0 1.4 %collective-permute-start = (bf16[64,2048]{1,0:T(8,128)(2,1)}, bf16[64,2048]{1,0:T(8,128)(2,1)}, u32[]{:S(2)}, u32[]{:S(2)}) collective-permute-start(bf16[64,2048]{1,0:T(8,128)(2,1)} %bitcast.17), channel_id=1, source_target_pairs={{0,1},{1,0},{2,3},{3,2},{4,5},{5,4},{6,7},{7,6},{8,9},{9,8},{10,11... | collective-permute-start | bytes 786440 | tf_op jit(solution)/shard_map/ppermute | solution.py:365
  1.4 1.2 %collective-permute-done.xp_hbm = bf16[64,2048]{1,0:T(8,128)(2,1)} collective-permute-done((bf16[64,2048]{1,0:T(8,128)(2,1)}, bf16[64,2048]{1,0:T(8,128)(2,1)}, u32[]{:S(2)}, u32[]{:S(2)}) %collective-permute-start) | collective-permute-done | bytes 262176 | tf_op jit(solution)/shard_map/ppermute | solution.py:365
  2.5 104.3 %layer.1 = (bf16[64,2048]{1,0:T(8,128)(2,1)}, f32[64,2048]{1,0:T(8,128)}) custom-call(bf16[64,2048]{1,0:T(8,128)(2,1)} %bitcast.18, bf16[64,2048]{1,0:T(8,128)(2,1)} %collective-permute-done.xp_hbm, s32[8,64]{1,0:T(8,128)} %bitcast.21, f32[8,64]{1,0:T(8,128)} %bitcast.22, f32[1,2048]{1,0:T(1,128)} %bitcast.19, f32[1,2048]{1,0:T(1,128)} %bitcast.20, ...), custom_call_target="tpu_custom_call" | custom-call | tf_op jit(solution)/shard_map/layer/pallas_call | solution.py:334
  106.8 1.9 %fusion = bf16[1,64,2048]{2,1,0:T(8,128)(2,1)} fusion(f32[64,2048]{1,0:T(8,128)} %get-tuple-element.8, bf16[64,2048]{1,0:T(8,128)(2,1)} %get-tuple-element.7), kind=kLoop, calls=%fused_computation.1 | loop fusion | flops 393216 | bytes 1048576 | tf_op jit(solution)/shard_map/broadcast_in_dim | solution.py:368
Async XLA Ops:
  0.0 2.5 %collective-permute-start = (bf16[64,2048]{1,0:T(8,128)(2,1)}, bf16[64,2048]{1,0:T(8,128)(2,1)}, u32[]{:S(2)}, u32[]{:S(2)}) collective-permute-start(bf16[64,2048]{1,0:T(8,128)(2,1)} %bitcast.17), channel_id=1, source_target_pairs={{0,1},{1,0},{2,3},{3,2},{4,5},{5,4},{6,7},{7,6},{8,9},{9,8},{10,11... | collective-permute-start | bytes 786440 | tf_op jit(solution)/shard_map/ppermute | solution.py:365

commit v4 on v3

--- a/solution.py
+++ b/solution.py
@@ -56,7 +56,7 @@
 
 
 def layer_kernel(n, cap, top,
-                 x_hbm, xp_hbm, idx_hbm, gate_ref, g1_hbm, g2_hbm, wq, wk, wv, wo, w1, w3, w2,
+                 x_hbm, idx_hbm, gate_ref, g1_hbm, g2_hbm, wq, wk, wv, wo, w1, w3, w2,
                  hv, moe_ref,
                  xv, idxv, g1v, g2v, bq, bk, bv, bo, e1, e3, e2,
                  xn, acc, part, tokv, dstv, toks, dsts,
@@ -88,7 +88,6 @@
 
     ins = [
         pltpu.make_async_copy(x_hbm, xv.at[:t_len], in_sem.at[0]),
-        pltpu.make_async_copy(xp_hbm, xv.at[t_len:], in_sem.at[4]),
         pltpu.make_async_copy(idx_hbm, idxv, in_sem.at[1]),
         pltpu.make_async_copy(g1_hbm, g1v, in_sem.at[2]),
         pltpu.make_async_copy(g2_hbm, g2v, in_sem.at[3]),
@@ -139,8 +138,15 @@
     for cp in tables:
         cp.start()
 
-    xn[...] = rms(xv[...].astype(jnp.float32), g1v[...])
+    xn[:t_len] = rms(xv[:t_len].astype(jnp.float32), g1v[...])
     acc[...] = jnp.zeros_like(acc)
+    pl.semaphore_wait(barrier, n - 1)
+    meet = pltpu.make_async_remote_copy(
+        src_ref=xv.at[:t_len], dst_ref=xv.at[t_len:], send_sem=p_ssem.at[0], recv_sem=p_rsem.at[0],
+        device_id={'ep': mate}, device_id_type=MESH)
+    meet.start()
+    meet.wait()
+    xn[t_len:] = rms(xv[t_len:].astype(jnp.float32), g1v[...])
     row = lax.broadcasted_iota(jnp.int32, (t2, t2), 0)
     col = lax.broadcasted_iota(jnp.int32, (t2, t2), 1)
     keep = (row >= col) & (row // t_len == col // t_len)
@@ -179,9 +185,8 @@
 
     lax.fori_loop(0, groups, group, 0)
 
-    pl.semaphore_wait(barrier, n - 1)
     swap = pltpu.make_async_remote_copy(
-        src_ref=acc.at[t_len:], dst_ref=part, send_sem=p_ssem, recv_sem=p_rsem,
+        src_ref=acc.at[t_len:], dst_ref=part, send_sem=p_ssem.at[1], recv_sem=p_rsem.at[1],
         device_id={'ep': mate}, device_id_type=MESH)
     swap.start()
     swap.wait()
@@ -302,14 +307,16 @@
     for p in range(passes):
         full(p, esend, back, ret_ssem.at[p], ret_rsem.at[p]).wait_recv()
 
-    def combine(t, carry):
-        total = jnp.zeros((kb, LANES), jnp.float32)
-        for j in range(top):
-            total = total + back[dsts[j, t]].astype(jnp.float32) * gate_ref[j, t]
-        moe32[t] = total
+    def combine(k, carry):
+        for s in range(4):
+            t = 4 * k + s
+            total = jnp.zeros((kb, LANES), jnp.float32)
+            for j in range(top):
+                total = total + back[dsts[j, t]].astype(jnp.float32) * gate_ref[j, t]
+            moe32[t] = total
         return carry
 
-    lax.fori_loop(0, t_len, combine, 0)
+    lax.fori_loop(0, t_len // 4, combine, 0)
     for b in range(kb):
         moe_ref[:, b * LANES:(b + 1) * LANES] = moe32[:, b, :]
 
@@ -318,7 +325,7 @@
         full(p, esend, back, ret_ssem.at[p], ret_rsem.at[p]).wait_send()
 
 
-def layer(n, x, xp, idx, gates, g1, g2, wq, wk, wv, wo, w1, w3, w2):
+def layer(n, x, idx, gates, g1, g2, wq, wk, wv, wo, w1, w3, w2):
     t_len, d = x.shape
     top = idx.shape[0]
     avg = top * t_len // n
@@ -334,7 +341,7 @@
     return pl.pallas_call(
         functools.partial(layer_kernel, n, cap, top),
         out_shape=(jax.ShapeDtypeStruct((t_len, d), bf), jax.ShapeDtypeStruct((t_len, d), f32)),
-        in_specs=[anyspec, anyspec, anyspec, pl.BlockSpec(memory_space=pltpu.SMEM)] + [anyspec] * 9,
+        in_specs=[anyspec, anyspec, pl.BlockSpec(memory_space=pltpu.SMEM)] + [anyspec] * 9,
         out_specs=(pl.BlockSpec(memory_space=pltpu.VMEM), pl.BlockSpec(memory_space=pltpu.VMEM)),
         scratch_shapes=[
             V((2 * t_len, d), bf), V((top, t_len), i32), V((1, d), f32), V((1, d), f32),
@@ -345,13 +352,13 @@
             V((max(rows, t_len), kb, LANES), f32), V((t_len, kb, LANES), bf),
             V((n * cap, kb, LANES), bf), V((n * cap, kb, LANES), bf), V((rows, d), bf),
             V((n * cap, kb, LANES), bf), V((n * cap, kb, LANES), bf), V((t_len, kb, LANES), f32),
-            DMA((5,)), DMA((NBUF, 4)), DMA((3,)), DMA((2,)), DMA, DMA,
+            DMA((4,)), DMA((NBUF, 4)), DMA((3,)), DMA((2,)), DMA((2,)), DMA((2,)),
             DMA((passes,)), DMA((passes * PARTS,)), DMA((passes,)), DMA((passes,)),
         ],
         compiler_params=pltpu.CompilerParams(
             collective_id=0, has_side_effects=True, vmem_limit_bytes=67043328),
         name='layer',
-    )(x, xp, idx, gates, g1, g2, wq, wk, wv, wo, w1, w3, w2)
+    )(x, idx, gates, g1, g2, wq, wk, wv, wo, w1, w3, w2)
 
 
 def solution(mesh):
@@ -362,8 +369,7 @@
 
     def body(x, idx, gates, g1, wq, wk, wv, wo, g2, w1, w3, w2):
         d = x.shape[-1]
-        xp = lax.ppermute(x[0], 'ep', [(i, i ^ 1) for i in range(n)])
-        h, moe = layer(n, x[0], xp, idx[0].T, gates[0].T, g1.reshape(1, d), g2.reshape(1, d),
+        h, moe = layer(n, x[0], idx[0].T, gates[0].T, g1.reshape(1, d), g2.reshape(1, d),
                   wq, wk, wv, wo, w1[0], w3[0], w2[0])
         return (h.astype(jnp.float32) + moe).astype(jnp.bfloat16)[None]
 

time: 109 us -> 107 us (0.982)
  starting transfers between devices: 1.36 us -> 0 us
  waiting for transfers between devices: 1.16 us -> 0 us
    ppermute x1 -> x0, starting transfers between devices: 1.36 us -> none  [body(): xp = lax.ppermute(x[0], 'ep', [(i, i ^ 1) for i in range(n)])]
    pallas_call x1, Pallas kernels: 104 us -> 105 us  [layer(): pl.pallas_call(functools.partial(layer_kernel, n, cap, top), out_shape=(j...]
    ppermute x1 -> x0, waiting for transfers between devices: 1.16 us -> none  [body(): xp = lax.ppermute(x[0], 'ep', [(i, i ^ 1) for i in range(n)])]
  transfers between devices with their start and end apart: 1 -> 0, of which waited for: 1 -> 0; matrix products, arithmetic and copies ran while one was open for 0% -> 0% of each run, Pallas kernels for 0% -> 0%
where the time goes in v4:
time: 107 us
  Pallas kernels  105 us (98%)
  other arithmetic  1.86 us (2%)
    pallas_call x1, Pallas kernels, layer(): pl.pallas_call(functools.partial(layer_kernel, n, cap, top), out_shape=(j...  105 us

profile of v4, /device:TPU:1, one launch (start us, length us, event | category | flops | bytes accessed | tf_op | source)
XLA Modules:
  0.0 107.3 jit_solution(9602541974311098200)
XLA Ops:
  0.0 105.5 %layer.1 = (bf16[64,2048]{1,0:T(8,128)(2,1)}, f32[64,2048]{1,0:T(8,128)}) custom-call(bf16[64,2048]{1,0:T(8,128)(2,1)} %bitcast.17, s32[8,64]{1,0:T(8,128)} %bitcast.20, f32[8,64]{1,0:T(8,128)} %bitcast.21, f32[1,2048]{1,0:T(1,128)} %bitcast.18, f32[1,2048]{1,0:T(1,128)} %bitcast.19, bf16[2048,4096]{1,0:T(8,128)(2,1)} %wq.1, bf16[2048,4096]{1,0:T(8,128)(2,1)} %wk.1, ...), custom_call_target="tpu_custom_call" | custom-call | tf_op jit(solution)/shard_map/layer/pallas_call | solution.py:341
  105.5 1.9 %fusion = bf16[1,64,2048]{2,1,0:T(8,128)(2,1)} fusion(f32[64,2048]{1,0:T(8,128)} %get-tuple-element.8, bf16[64,2048]{1,0:T(8,128)(2,1)} %get-tuple-element.7), kind=kLoop, calls=%fused_computation.1 | loop fusion | flops 393216 | bytes 1048576 | tf_op jit(solution)/shard_map/broadcast_in_dim | solution.py:374
